TPU v7x, 32 devices: a whole 2x2x4 slice. The times are simulated.
32 devices in a mesh: head: 8 (over y, x, core), level: 4 (over z).
Axes of the slice: x: 2, y: 2, z: 4, core: 2. Of those that a mesh axis runs over, the one named last changes fastest.
Arguments:
- features: float32 [64, 4096], P(None, ('head', 'level')), may hold values from -6 to 6
- in_gain: float32 [4096], replicated, may hold values from 0.25 to 1.75
- in_weight: bfloat16 [4096, 4288], P(None, 'head'), may hold values from -0.09375 to 0.09375
- level_bias: float32 [8, 24], P('head'), may hold values from -4 to 252
- states: bfloat16 [64, 8, 24, 128, 128], P(None, 'head', 'level'), may hold values from -1.25 to 1.25
- positions: int32 [64], replicated, may hold values from 1 to 262143
- out_gain: float32 [1024], P('head'), may hold values from 0.25 to 1.75
- out_weight: bfloat16 [1024, 4096], P('head', 'level'), may hold values from -0.1875 to 0.1875
Outputs:
- output: float32 [64, 4096], P('head', 'level')
Inputs may be any that keep to these rules, and one draw needn't show every extreme that they name: `positions`: positions below 2 ** 18, so levels from 19 on are never occupied.
All inputs are finite; a program needn't handle non-finite values.
Results may differ from a plain program's by a relative error of at most 0.0066.
Values sent between devices are 32-bit elements; how exact they have to be, the bound alone decides.
A program may use at most 64 MiB of HBM per device.

v0:
```python
import jax
import jax.numpy as jnp
from jax import lax
from jax.sharding import PartitionSpec as P


def folder(weight_rows, gain_rows, shard_part):
    scaled = (shard_part * gain_rows).astype(jnp.bfloat16)
    product = jnp.dot(scaled, weight_rows, preferred_element_type=jnp.float32)
    return (product, jnp.sum(shard_part * shard_part, axis=1))


def occupancy(positions, level_ids):
    shifted = jnp.right_shift(positions[:, None], jnp.maximum(level_ids - 1, 0)[None, :])
    bits = jnp.bitwise_and(shifted, 1)
    first = (level_ids[None, :] == 0).astype(jnp.int32)
    return jnp.maximum(first, bits)[:, None, :]


def body(features, in_gain, in_weight, level_bias, states, positions, out_gain, out_weight):
    seq_count = features.shape[0]
    width = in_gain.shape[0]
    head_here = level_bias.shape[0]
    level_total = level_bias.shape[1]
    level_here = states.shape[2]
    key_dim = states.shape[3]
    val_dim = states.shape[4]
    proj_cols = in_weight.shape[1] // head_here
    level_index = lax.axis_index("level")
    proj_sum, squares = folder(
        in_weight, in_gain, lax.all_gather(features, ("head", "level"), axis=1, tiled=True)
    )
    row_scale = lax.rsqrt(squares / width + 1e-06)
    projected = (proj_sum * row_scale[:, None]).reshape(seq_count, head_here, proj_cols)
    query_vec = projected[:, :, :key_dim]
    key_vec = projected[:, :, key_dim : 2 * key_dim]
    value_vec = projected[:, :, 2 * key_dim : 2 * key_dim + val_dim]
    gate_vec = projected[:, :, 2 * key_dim + val_dim : 2 * key_dim + 2 * val_dim]
    logits = projected[:, :, 2 * key_dim + 2 * val_dim :] + level_bias[None]
    local_ids = level_index * level_here + jnp.arange(level_here, dtype=jnp.int32)
    query_low = query_vec.astype(jnp.bfloat16)
    reads = jnp.einsum("bhk,bhlkv->bhlv", query_low, states, preferred_element_type=jnp.float32)
    own_term = jnp.sum(query_vec * key_vec, axis=2, keepdims=True) * key_dim ** (-0.5) * value_vec
    first_level = (local_ids == 0).astype(jnp.float32)
    all_occupied = occupancy(positions, jnp.arange(level_total, dtype=jnp.int32)) == 1
    peak_logit = jnp.max(jnp.where(all_occupied, logits, -1e30), axis=2, keepdims=True)
    all_weights = jnp.where(all_occupied, jnp.exp(logits - peak_logit), 0.0)
    total_weight = jnp.sum(all_weights, axis=2)
    local_weights = lax.dynamic_slice_in_dim(all_weights, level_index * level_here, level_here, 2)
    mixture = (
        jnp.sum(local_weights[..., None] * reads, axis=2)
        + jnp.sum(local_weights * first_level, axis=2)[..., None] * own_term
    )
    mixed = lax.psum(mixture, "level")
    level_out = mixed / total_weight[..., None]
    gated = (level_out * jax.nn.silu(gate_vec)).reshape(seq_count, head_here * val_dim)
    square_sum = lax.psum(jnp.sum(gated * gated, axis=1), "head")
    feature_count = lax.axis_size("head") * head_here * val_dim
    normed = (gated * lax.rsqrt(square_sum / feature_count + 1e-05)[:, None] * out_gain).astype(
        jnp.bfloat16
    )
    return lax.psum_scatter(
        jnp.dot(normed, out_weight, preferred_element_type=jnp.float32),
        "head",
        scatter_dimension=0,
        tiled=True,
    )


def solution(mesh):
    in_specs = (
        P(None, ("head", "level")),
        P(),
        P(None, "head"),
        P("head", None),
        P(None, "head", "level", None, None),
        P(),
        P("head"),
        P("head", "level"),
    )
    out_specs = P("head", "level")
    return jax.shard_map(body, mesh=mesh, in_specs=in_specs, out_specs=out_specs, check_vma=False)
```

profile of v0, /device:TPU:0, one launch (start us, length us, event | category | flops | bytes accessed | tf_op | source)
XLA Modules:
  0.0 148.1 jit_solution(14782382644225926539)
XLA Ops:
  6.5 0.0 copy-start
  6.5 0.0 all-gather.2.cloned.1.call-start
  6.5 0.7 all-gather.2.cloned.1.call-update
  7.3 0.0 reduce-scatter.2.cloned.1.call-start
  7.3 57.9 %all-gather.2.cloned.1.call-done = f32[64,4096]{1,0:T(8,128)} async-done(((f32[64,128]{1,0:T(8,128)}), f32[64,4096]{1,0:T(8,128)}) %all-gather.2.cloned.1.call-update) | async-done | bytes 1048592 | tf_op jit(solution)/shard_map/all_gather | solution.py:31
  65.3 1.4 multiply_reduce_fusion
  66.7 0.0 copy-start.1
  66.7 4.1 %fusion.2 = f32[64,1,536]{2,0,1:T(8,128)S(1)} fusion(bf16[4096,536]{0,1:T(8,128)(2,1)} %param.10, f32[64,4096]{1,0:T(8,128)} %all-gather.2.cloned.1.call-done, f32[4096]{0:T(1024)} %param.9, f32[64]{0:T(128)S(1)} %add_rsqrt_fusion.1), kind=kOutput, calls=%fused_computation.3 | convolution fusion | flops 281576960 | bytes 5593344 | tf_op jit(solution)/shard_map/dot_general | solution.py:9
  70.8 0.1 fusion.7
  70.9 0.9 select_reduce_fusion
  71.8 0.9 fusion.17
  72.7 0.2 multiply_reduce_fusion.1
  72.9 0.1 copy.9
  72.9 6.3 %fusion = f32[64,1,6,128]{3,1,2,0:T(1,128)S(1)} fusion(bf16[64,1,6,128,128]{4,3,2,1,0:T(8,128)(2,1)} %param.12, bf16[64,128,1,1]{1,0,2,3:T(8,128)(2,1)S(1)} %fusion.12), kind=kOutput, calls=%fused_computation | convolution fusion | flops 12582912 | bytes 12795904 | tf_op jit(solution)/shard_map/bhk,bhlkv->bhlv/dot_general | solution.py:42
  79.3 0.1 fusion.4
  79.4 0.1 fusion.6
  79.5 17.4 %psum.14 = f32[64,1,128]{2,0,1:T(8,128)S(1)} all-reduce(f32[64,1,128]{2,0,1:T(8,128)S(1)} %fusion.6), channel_id=1, replica_groups=mesh['head'=8,'level'=4] {'level'}, use_global_device_ids=true, to_apply=%region_5.6 | all-reduce | flops 8192 | bytes 65536 | tf_op jit(solution)/shard_map/psum | solution.py:54
  96.9 0.2 fusion.8
  97.1 11.8 %psum.15 = f32[64]{0:T(128)S(1)} all-reduce(f32[64]{0:T(128)S(1)} %get-tuple-element.5), channel_id=1, replica_groups=mesh['head'=8,'level'=4] {'head'}, use_global_device_ids=true, to_apply=%region_8.9 | all-reduce | flops 64 | bytes 512 | tf_op jit(solution)/shard_map/psum | solution.py:57
  108.9 0.0 copy-done
  108.9 0.0 copy-done.1
  108.9 0.9 fusion.13
  109.8 0.0 reduce-scatter.2.cloned.1.call-update
  109.9 31.4 %reduce-scatter.2.cloned.1.call-done = f32[8,1024]{1,0:T(8,128)} async-done(((f32[64,1024]{1,0:T(8,128)}), f32[8,1024]{1,0:T(8,128)}) %reduce-scatter.2.cloned.1.call-update) | async-done | bytes 32784 | tf_op jit(solution)/shard_map/reduce_scatter | solution.py:62
  (7 shorter events, 0.0 us)
Async XLA Ops:
  6.5 102.4 %copy-start = (bf16[128,1024]{1,0:T(8,128)(2,1)S(1)}, bf16[128,1024]{1,0:T(8,128)(2,1)}, u32[]{:S(2)}) copy-start(bf16[128,1024]{1,0:T(8,128)(2,1)} %param.15) | copy-start | bytes 786436
  6.5 58.8 %all-gather.2.cloned.1.call-start = ((), (), s32[]{:S(2)}) async-start(), calls=%async_computation.1 | async-start | bytes 1081344 | tf_op jit(solution)/shard_map/all_gather | solution.py:31
  7.3 134.0 %reduce-scatter.2.cloned.1.call-start = ((), (), s32[]{:S(2)}) async-start(), calls=%async_computation.2 | async-start | bytes 294912 | tf_op jit(solution)/shard_map/reduce_scatter | solution.py:62
  66.7 42.2 %copy-start.1 = (f32[128]{0:T(128)S(1)}, f32[128]{0:T(128)}, u32[]{:S(2)}) copy-start(f32[128]{0:T(128)} %param.14) | copy-start | bytes 1540
Sparse Core Ops, SparseCore 0:
  10.2 55.0 all-gather.1
  110.0 31.1 reduce-scatter.1
where the time goes:
time: 148 us
  waiting for transfers between devices  90 us (61%)
  blocking collectives  29.2 us (20%)
  between operations  13.5 us (9%)
  matrix products  11.4 us (8%)
  other arithmetic  3.82 us (3%)
    all_gather x1, waiting for transfers between devices, body(): lax.all_gather(features, ('head', 'level'), axis=1, tiled=True)  57.9 us
    reduce_scatter x1, waiting for transfers between devices, body(): lax.psum_scatter(jnp.dot(normed, out_weight, preferred_element_type=jnp.f...  31.4 us
    psum x1, blocking collectives, body(): mixed = lax.psum(mixture, 'level')  17.4 us
    psum x1, blocking collectives, body(): square_sum = lax.psum(jnp.sum(gated * gated, axis=1), 'head')  11.8 us
    dot_general x1, matrix products, body(): jnp.einsum('bhk,bhlkv->bhlv', query_low, states, preferred_element_type=j...  6.33 us
    dot_general x1, matrix products, folder(): product = jnp.dot(scaled, weight_rows, preferred_element_type=jnp.float32)  4.1 us
  transfers between devices with their start and end apart: 2, of which 2 were waited for; matrix products, arithmetic and copies ran while one was open for 0% of the time, Pallas kernels for 0%

commit v1 on v0

v1 whole, which is shorter than its diff:
```python
import functools

import jax
import jax.numpy as jnp
from jax import lax
from jax.experimental import pallas as pl
from jax.experimental.pallas import tpu as pltpu
from jax.sharding import PartitionSpec as P

LANES = 128
GROUP = 16


def send(src, dst, send_sem, recv_sem, target):
    return pltpu.make_async_remote_copy(
        src_ref=src,
        dst_ref=dst,
        send_sem=send_sem,
        recv_sem=recv_sem,
        device_id=target,
        device_id_type=pl.DeviceIdType.MESH,
    )


def kernel(
    heads, levels, width, dims,
    feat, gain, inw, bias, states, pos, ogain, outw, out,
    xbuf, wbuf, sbuf, owbuf, proj, abuf, bbuf, mbuf, osend, orecv, qfull, wnorm, qw, biasbuf,
    x_sem, w_sem, s_sem, ow_sem, p1_send, p1_recv, a_send, a_recv, b_send, b_recv,
    m_send, m_recv, o_send, o_recv,
):
    key_dim, val_dim, level_total, level_here = dims
    seqs, fw = feat.shape
    flipped = fw % LANES == 0
    cols = inw.shape[0] if flipped else inw.shape[1]
    owned = seqs // levels
    out_rows = seqs // heads
    out_cols = outw.shape[1]
    me_h, me_l = lax.axis_index("head"), lax.axis_index("level")
    slot = 1 << level_total.bit_length()
    slots = LANES // slot
    packed = seqs // slots
    groups = seqs // GROUP

    x_copy = pltpu.make_async_copy(feat, xbuf.at[me_h], x_sem)
    x_copy.start()
    w_copies = []
    for h in range(heads):
        start = pl.multiple_of((h * levels + me_l) * fw, fw)
        part = inw.at[:, pl.ds(start, fw)] if flipped else inw.at[pl.ds(start, fw), :]
        w_copies.append(pltpu.make_async_copy(part, wbuf.at[h], w_sem.at[h]))
        w_copies[-1].start()
    s_copies = []
    for g in range(groups):
        rows = pl.ds(g * GROUP, GROUP)
        s_copies.append(pltpu.make_async_copy(states.at[rows], sbuf.at[rows], s_sem.at[g]))
        s_copies[-1].start()
    ow_copy = pltpu.make_async_copy(outw, owbuf, ow_sem)
    ow_copy.start()

    barrier = pltpu.get_barrier_semaphore()
    for o in range(1, heads):
        pl.semaphore_signal(
            barrier, inc=1, device_id=(lax.rem(me_h + o, heads), me_l),
            device_id_type=pl.DeviceIdType.MESH)
    for o in range(1, levels):
        pl.semaphore_signal(
            barrier, inc=1, device_id=(me_h, lax.rem(me_l + o, levels)),
            device_id_type=pl.DeviceIdType.MESH)
    pl.semaphore_wait(barrier, heads + levels - 2)

    x_copy.wait()
    pending = []
    for o in range(1, heads):
        peer = lax.rem(me_h + o, heads)
        c = send(xbuf.at[me_h], xbuf.at[me_h], p1_send.at[o], p1_recv.at[me_h], (peer, me_l))
        c.start()
        pending.append(c)

    for c in w_copies:
        c.wait()
    acc = jnp.zeros((seqs, cols), jnp.float32)
    squares = jnp.zeros((seqs, 1), jnp.float32)
    for o in range(heads):
        src = lax.rem(me_h + heads - o, heads)
        if o:
            send(xbuf.at[src], xbuf.at[src], p1_send.at[o], p1_recv.at[src], (src, me_l)).wait_recv()
        x = xbuf[src]
        g = gain[pl.ds(src * levels + me_l, 1), :]
        acc += lax.dot_general(
            (x * g).astype(jnp.bfloat16), wbuf[src], (((1,), (1 if flipped else 0,)), ((), ())),
            preferred_element_type=jnp.float32)
        squares += jnp.sum(x * x, axis=1, keepdims=True)

    proj[:, :cols] = acc
    lane = lax.broadcasted_iota(jnp.int32, (seqs, LANES), 1)
    tail0 = 2 * key_dim + 2 * val_dim
    tail = jnp.where(lane < level_total, proj[:, tail0 : tail0 + LANES], 0.0)
    tail = jnp.where(lane == level_total, squares, tail)
    pack = tail[:packed]
    for c in range(1, slots):
        pack += pltpu.roll(tail[c * packed : (c + 1) * packed], slot * c, 1)
    abuf[me_l, :seqs, :] = acc[:, :key_dim]
    abuf[me_l, seqs:, :] = pack
    for o in range(1, levels):
        peer = lax.rem(me_l + o, levels)
        c = send(abuf.at[me_l], abuf.at[me_l], a_send.at[o], a_recv.at[me_l], (me_h, peer))
        c.start()
        pending.append(c)
    for o in range(1, levels):
        peer = lax.rem(me_l + o, levels)
        rows = pl.ds(pl.multiple_of(peer * owned, owned), owned)
        c = send(proj.at[rows, pl.ds(key_dim, tail0 - key_dim)], bbuf.at[me_l],
                 b_send.at[o], b_recv.at[me_l], (me_h, peer))
        c.start()
        pending.append(c)
    mine = pl.ds(pl.multiple_of(me_l * owned, owned), owned)
    bbuf[me_l] = proj[mine, key_dim:tail0]

    biasbuf[:, :level_total] = bias[...]
    row = lax.broadcasted_iota(jnp.int32, (seqs, seqs), 0)
    col = lax.broadcasted_iota(jnp.int32, (seqs, seqs), 1)
    pos_f = jnp.broadcast_to(pos[...], (seqs, seqs)).astype(jnp.float32)
    pos_col = jnp.sum(jnp.where(row == col, pos_f, 0.0), axis=1, keepdims=True).astype(jnp.int32)
    shift = jnp.clip(lane - 1, 0, 31)
    bits = jnp.bitwise_and(jnp.right_shift(jnp.broadcast_to(pos_col, lane.shape), shift), 1)
    occupied = jnp.logical_and(lane < level_total, jnp.logical_or(lane == 0, bits == 1))

    for o in range(1, levels):
        src = lax.rem(me_l + levels - o, levels)
        send(abuf.at[src], abuf.at[src], a_send.at[o], a_recv.at[src], (me_h, src)).wait_recv()
    query = abuf[0, :seqs, :]
    pack = abuf[0, seqs:, :]
    for l in range(1, levels):
        query += abuf[l, :seqs, :]
        pack += abuf[l, seqs:, :]
    parts = [pack] + [pltpu.roll(pack, LANES - slot * c, 1) for c in range(1, slots)]
    tail = jnp.concatenate(parts, axis=0)
    row_scale = lax.rsqrt(tail[:, level_total : level_total + 1] / width + 1e-06)
    query = query * row_scale
    logits = tail * row_scale + biasbuf[...]
    peak = jnp.max(jnp.where(occupied, logits, -1e30), axis=1, keepdims=True)
    weights = jnp.where(occupied, jnp.exp(logits - peak), 0.0)
    weights = weights / jnp.sum(weights, axis=1, keepdims=True)
    qfull[...] = query
    wnorm[:, :LANES] = weights
    wnorm[:, LANES:] = jnp.broadcast_to(row_scale, weights.shape)
    local = pltpu.roll(weights, lax.rem(LANES - me_l * level_here, LANES), 1)
    query_low = query.astype(jnp.bfloat16).astype(jnp.float32)
    for j in range(level_here):
        qw[:, j * key_dim : (j + 1) * key_dim] = (query_low * local[:, j : j + 1]).astype(jnp.bfloat16)

    seq_in = lax.broadcasted_iota(jnp.int32, (GROUP, val_dim), 0)
    for g in range(groups):
        s_copies[g].wait()
    def read_group(g, carry):
        base = pl.multiple_of(g * GROUP, GROUP)
        left = qw[pl.ds(base, GROUP), :]
        mixed = jnp.zeros((GROUP, val_dim), jnp.float32)
        for i in range(GROUP):
            got = jnp.dot(left, sbuf[base + i], preferred_element_type=jnp.float32)
            mixed = jnp.where(seq_in == i, got, mixed)
        mbuf[me_l, pl.ds(base, GROUP), :] = mixed
        return carry
    lax.fori_loop(0, groups, read_group, 0)

    for o in range(1, levels):
        src = lax.rem(me_l + levels - o, levels)
        send(bbuf.at[src], bbuf.at[src], b_send.at[o], b_recv.at[src], (me_h, src)).wait_recv()
    rest = bbuf[0]
    for l in range(1, levels):
        rest += bbuf[l]
    rest = rest * wnorm[mine, LANES : LANES + 1]
    key, value = rest[:, :key_dim], rest[:, key_dim : key_dim + val_dim]
    gate = rest[:, key_dim + val_dim :]
    own = jnp.sum(qfull[mine, :] * key, axis=1, keepdims=True) * key_dim ** (-0.5) * value
    mbuf[me_l, mine, :] = mbuf[me_l, mine, :] + wnorm[mine, 0:1] * own
    mbuf[me_l, seqs:, :] = gate * jax.nn.sigmoid(gate)
    for o in range(1, levels):
        peer = lax.rem(me_l + o, levels)
        c = send(mbuf.at[me_l], mbuf.at[me_l], m_send.at[o], m_recv.at[me_l], (me_h, peer))
        c.start()
        pending.append(c)
    ow_copy.wait()
    for o in range(1, levels):
        src = lax.rem(me_l + levels - o, levels)
        send(mbuf.at[src], mbuf.at[src], m_send.at[o], m_recv.at[src], (me_h, src)).wait_recv()
    gated = mbuf[0, :seqs, :]
    for l in range(1, levels):
        gated += mbuf[l, :seqs, :]
    gated = gated * jnp.concatenate([mbuf[l, seqs:, :] for l in range(levels)], axis=0)
    total_sq = jnp.sum(gated * gated, axis=1, keepdims=True)
    product = jnp.dot((gated * ogain[...]).astype(jnp.bfloat16), owbuf[...], preferred_element_type=jnp.float32)
    wide_sq = jnp.broadcast_to(total_sq, (seqs, LANES))
    for h in range(heads):
        osend[h, :, :out_cols] = product[h * out_rows : (h + 1) * out_rows]
        osend[h, :, out_cols:] = wide_sq[h * out_rows : (h + 1) * out_rows]
    for o in range(1, heads):
        peer = lax.rem(me_h + o, heads)
        c = send(osend.at[peer], orecv.at[me_h], o_send.at[o], o_recv.at[me_h], (peer, me_l))
        c.start()
        pending.append(c)
    total = osend[me_h]
    for o in range(1, heads):
        src = lax.rem(me_h + heads - o, heads)
        send(osend.at[src], orecv.at[src], o_send.at[o], o_recv.at[src], (src, me_l)).wait_recv()
        total += orecv[src]
    mean = total[:, out_cols : out_cols + 1] / (heads * val_dim)
    out[...] = total[:, :out_cols] * lax.rsqrt(mean + 1e-05)
    for c in pending:
        c.wait_send()


def body(features, in_gain, in_weight, level_bias, states, positions, out_gain, out_weight):
    heads, levels = lax.axis_size("head"), lax.axis_size("level")
    seqs, fw = features.shape
    cols = in_weight.shape[1]
    _, head_here, level_here, key_dim, val_dim = states.shape
    level_total = level_bias.shape[1]
    assert head_here == 1 and key_dim == LANES and val_dim == LANES
    out_cols = out_weight.shape[1]
    flipped = fw % LANES == 0
    slots = LANES // (1 << level_total.bit_length())
    owned, out_rows = seqs // levels, seqs // heads
    f32, bf16 = jnp.float32, jnp.bfloat16
    vmem, anyspace = pl.BlockSpec(memory_space=pltpu.VMEM), pl.BlockSpec(memory_space=pl.ANY)
    dma = pltpu.SemaphoreType.DMA
    tail0 = 2 * key_dim + 2 * val_dim
    return pl.pallas_call(
        functools.partial(kernel, heads, levels, in_gain.shape[0], (key_dim, val_dim, level_total, level_here)),
        out_shape=jax.ShapeDtypeStruct((out_rows, out_cols), f32),
        in_specs=[anyspace, vmem, anyspace, vmem, anyspace, vmem, vmem, anyspace],
        out_specs=vmem,
        scratch_shapes=[
            pltpu.VMEM((heads, seqs, fw), f32),
            pltpu.VMEM((heads, cols, fw) if flipped else (heads, fw, cols), bf16),
            pltpu.VMEM((seqs, level_here * key_dim, val_dim), bf16),
            pltpu.VMEM(out_weight.shape, bf16),
            pltpu.VMEM((seqs, tail0 + LANES), f32),
            pltpu.VMEM((levels, seqs + seqs // slots, key_dim), f32),
            pltpu.VMEM((levels, owned, tail0 - key_dim), f32),
            pltpu.VMEM((levels, seqs + owned, val_dim), f32),
            pltpu.VMEM((heads, out_rows, out_cols + LANES), f32),
            pltpu.VMEM((heads, out_rows, out_cols + LANES), f32),
            pltpu.VMEM((seqs, key_dim), f32),
            pltpu.VMEM((seqs, 2 * LANES), f32),
            pltpu.VMEM((seqs, level_here * key_dim), bf16),
            pltpu.VMEM((1, LANES), f32),
            dma(()), dma((heads,)), dma((seqs // GROUP,)), dma(()),
            dma((heads,)), dma((heads,)),
            dma((levels,)), dma((levels,)), dma((levels,)), dma((levels,)),
            dma((levels,)), dma((levels,)),
            dma((heads,)), dma((heads,)),
        ],
        compiler_params=pltpu.CompilerParams(collective_id=0, has_side_effects=True),
    )(
        features,
        in_gain.reshape(heads * levels, fw),
        in_weight.T if flipped else in_weight,
        level_bias,
        states.reshape(seqs, level_here * key_dim, val_dim),
        positions.reshape(1, seqs),
        out_gain.reshape(1, val_dim),
        out_weight,
    )


def solution(mesh):
    in_specs = (
        P(None, ("head", "level")),
        P(),
        P(None, "head"),
        P("head", None),
        P(None, "head", "level", None, None),
        P(),
        P("head"),
        P("head", "level"),
    )
    out_specs = P("head", "level")
    return jax.shard_map(body, mesh=mesh, in_specs=in_specs, out_specs=out_specs, check_vma=False)
```

time: 148 us -> 33.3 us (0.22)
  waiting for transfers between devices: 90 us -> 0 us
  Pallas kernels: 0 us -> 31.7 us
  blocking collectives: 29.2 us -> 0 us
  between operations: 13.5 us -> 0.01 us
  matrix products: 11.4 us -> 0 us
  other arithmetic: 3.82 us -> 0 us
    all_gather x1 -> x0, waiting for transfers between devices: 57.9 us -> none  [body(): lax.all_gather(features, ('head', 'level'), axis=1, tiled=True)]
    pallas_call x0 -> x1, Pallas kernels: none -> 31.7 us  [body(): pl.pallas_call(functools.partial(kernel, heads, levels, in_gain.shape[0],...]
    reduce_scatter x1 -> x0, waiting for transfers between devices: 31.4 us -> none  [body(): lax.psum_scatter(jnp.dot(normed, out_weight, preferred_element_type=jnp.f...]
    psum x2 -> x0, blocking collectives: 29.2 us -> none  [the longest x1 17.4 us: body(): mixed = lax.psum(mixture, 'level')]
    dot_general x3 -> x0, matrix products: 11.4 us -> none  [the longest x1 6.33 us: body(): jnp.einsum('bhk,bhlkv->bhlv', query_low, states, preferred_element_type=j...]
    reduce_sum x6 -> x0, other arithmetic: 2.85 us -> none  [the longest x1 1.39 us: folder(): return (product, jnp.sum(shard_part * shard_part, axis=1))]
  transfers between devices with their start and end apart: 2 -> 0, of which waited for: 2 -> 0; matrix products, arithmetic and copies ran while one was open for 0% -> 0% of each run, Pallas kernels for 0% -> 0%
where the time goes in v1:
time: 33.3 us; the launch traced here: 33 us
  Pallas kernels  31.7 us (95%)
  local copies, waits for them, and re-layouts  1.38 us (4%)
    pallas_call x1, Pallas kernels, body(): pl.pallas_call(functools.partial(kernel, heads, levels, in_gain.shape[0],...  31.7 us
    unnamed x1, local copies, waits for them, and re-layouts  1.38 us

profile of v1, /device:TPU:0, one launch (start us, length us, event | category | flops | bytes accessed | tf_op | source)
XLA Modules:
  0.0 33.0 jit_solution(10004173671045651090)
XLA Ops:
  0.0 31.7 %shard_map.82 = f32[8,1024]{1,0:T(8,128)} custom-call(f32[64,128]{1,0:T(8,128)} %feat.1, f32[32,128]{1,0:T(8,128)} %bitcast.7, bf16[536,4096]{1,0:T(8,128)(2,1)} %bitcast.6, f32[1,24]{1,0:T(1,128)} %bias.1, bf16[64,768,128]{2,1,0:T(8,128)(2,1)} %bitcast.5, s32[1,64]{1,0:T(1,128)} %bitcast.8, f32[1,128]{1,0:T(1,128)} %bitcast.9, bf16[128,1024]{1,0:T(8,128)(2,1)} %outw.1), custom_call_target="tpu_custom_call" | custom-call | tf_op jit(solution)/shard_map/pallas_call | solution.py:229
  31.7 1.4 %copy.10 = f32[8,1024]{1,0:T(8,128)} copy(f32[8,1024]{1,0:T(8,128)} %shard_map.82) | data formatting | bytes 65536

commit v2 on v1

--- a/solution.py
+++ b/solution.py
@@ -50,13 +50,14 @@
         part = inw.at[:, pl.ds(start, fw)] if flipped else inw.at[pl.ds(start, fw), :]
         w_copies.append(pltpu.make_async_copy(part, wbuf.at[h], w_sem.at[h]))
         w_copies[-1].start()
-    s_copies = []
-    for g in range(groups):
-        rows = pl.ds(g * GROUP, GROUP)
-        s_copies.append(pltpu.make_async_copy(states.at[rows], sbuf.at[rows], s_sem.at[g]))
-        s_copies[-1].start()
+    last_group = (me_l * owned) // GROUP
+    order = [lax.rem(last_group + 1 + t, groups) for t in range(groups)]
+
+    def state_copy(g):
+        rows = pl.ds(pl.multiple_of(g * GROUP, GROUP), GROUP)
+        return pltpu.make_async_copy(states.at[rows], sbuf.at[rows], s_sem.at[g])
+
     ow_copy = pltpu.make_async_copy(outw, owbuf, ow_sem)
-    ow_copy.start()
 
     barrier = pltpu.get_barrier_semaphore()
     for o in range(1, heads):
@@ -71,26 +72,39 @@
 
     x_copy.wait()
     pending = []
-    for o in range(1, heads):
-        peer = lax.rem(me_h + o, heads)
-        c = send(xbuf.at[me_h], xbuf.at[me_h], p1_send.at[o], p1_recv.at[me_h], (peer, me_l))
+    buddy = me_h + 1 - 2 * lax.rem(me_h, 2)
+    def feature_send(block, target, index):
+        c = send(xbuf.at[block], xbuf.at[block], p1_send.at[index], p1_recv.at[block], (target, me_l))
         c.start()
         pending.append(c)
 
+    def feature_wait(block):
+        send(xbuf.at[block], xbuf.at[block], p1_send.at[0], p1_recv.at[block], (buddy, me_l)).wait_recv()
+
+    same = [lax.rem(me_h + o, heads) for o in range(2, heads, 2)]
+    for i, peer in enumerate(same):
+        feature_send(me_h, peer, i)
+    feature_send(me_h, buddy, heads - 1)
     for c in w_copies:
         c.wait()
     acc = jnp.zeros((seqs, cols), jnp.float32)
     squares = jnp.zeros((seqs, 1), jnp.float32)
-    for o in range(heads):
-        src = lax.rem(me_h + heads - o, heads)
-        if o:
-            send(xbuf.at[src], xbuf.at[src], p1_send.at[o], p1_recv.at[src], (src, me_l)).wait_recv()
+    other = [lax.rem(buddy + o, heads) for o in range(2, heads, 2)]
+    for i, src in enumerate([me_h, buddy] + same + other):
+        if i:
+            feature_wait(src)
+        if 2 <= i < 2 + len(same):
+            feature_send(src, buddy, len(same) + i - 2)
         x = xbuf[src]
         g = gain[pl.ds(src * levels + me_l, 1), :]
         acc += lax.dot_general(
             (x * g).astype(jnp.bfloat16), wbuf[src], (((1,), (1 if flipped else 0,)), ((), ())),
             preferred_element_type=jnp.float32)
         squares += jnp.sum(x * x, axis=1, keepdims=True)
+
+    for g in order:
+        state_copy(g).start()
+    ow_copy.start()
 
     proj[:, :cols] = acc
     lane = lax.broadcasted_iota(jnp.int32, (seqs, LANES), 1)
@@ -151,40 +165,49 @@
         qw[:, j * key_dim : (j + 1) * key_dim] = (query_low * local[:, j : j + 1]).astype(jnp.bfloat16)
 
     seq_in = lax.broadcasted_iota(jnp.int32, (GROUP, val_dim), 0)
-    for g in range(groups):
-        s_copies[g].wait()
-    def read_group(g, carry):
+    def to_levels(rows, index):
+        for o in range(1, levels):
+            part = mbuf.at[me_l, rows, :]
+            c = send(part, part, m_send.at[o, index], m_recv.at[me_l, index],
+                     (me_h, lax.rem(me_l + o, levels)))
+            c.start()
+            pending.append(c)
+
+    for t, g in enumerate(order):
+        if t == groups - 1:
+            for o in range(1, levels):
+                src = lax.rem(me_l + levels - o, levels)
+                send(bbuf.at[src], bbuf.at[src], b_send.at[o], b_recv.at[src], (me_h, src)).wait_recv()
+            rest = bbuf[0]
+            for l in range(1, levels):
+                rest += bbuf[l]
+            rest = rest * wnorm[mine, LANES : LANES + 1]
+            key, value = rest[:, :key_dim], rest[:, key_dim : key_dim + val_dim]
+            gate = rest[:, key_dim + val_dim :]
+            own = jnp.sum(qfull[mine, :] * key, axis=1, keepdims=True) * key_dim ** (-0.5) * value
+            mbuf[me_l, seqs:, :] = gate * jax.nn.sigmoid(gate)
+            to_levels(pl.ds(seqs, owned), groups)
+            qfull[...] = jnp.zeros(qfull.shape, jnp.float32)
+            qfull[mine, :] = wnorm[mine, 0:1] * own
+        state_copy(g).wait()
         base = pl.multiple_of(g * GROUP, GROUP)
-        left = qw[pl.ds(base, GROUP), :]
+        rows = pl.ds(base, GROUP)
+        left = qw[rows, :]
         mixed = jnp.zeros((GROUP, val_dim), jnp.float32)
         for i in range(GROUP):
             got = jnp.dot(left, sbuf[base + i], preferred_element_type=jnp.float32)
             mixed = jnp.where(seq_in == i, got, mixed)
-        mbuf[me_l, pl.ds(base, GROUP), :] = mixed
-        return carry
-    lax.fori_loop(0, groups, read_group, 0)
-
+        if t == groups - 1:
+            mixed += qfull[rows, :]
+        mbuf[me_l, rows, :] = mixed
+        to_levels(rows, g)
+    ow_copy.wait()
     for o in range(1, levels):
         src = lax.rem(me_l + levels - o, levels)
-        send(bbuf.at[src], bbuf.at[src], b_send.at[o], b_recv.at[src], (me_h, src)).wait_recv()
-    rest = bbuf[0]
-    for l in range(1, levels):
-        rest += bbuf[l]
-    rest = rest * wnorm[mine, LANES : LANES + 1]
-    key, value = rest[:, :key_dim], rest[:, key_dim : key_dim + val_dim]
-    gate = rest[:, key_dim + val_dim :]
-    own = jnp.sum(qfull[mine, :] * key, axis=1, keepdims=True) * key_dim ** (-0.5) * value
-    mbuf[me_l, mine, :] = mbuf[me_l, mine, :] + wnorm[mine, 0:1] * own
-    mbuf[me_l, seqs:, :] = gate * jax.nn.sigmoid(gate)
-    for o in range(1, levels):
-        peer = lax.rem(me_l + o, levels)
-        c = send(mbuf.at[me_l], mbuf.at[me_l], m_send.at[o], m_recv.at[me_l], (me_h, peer))
-        c.start()
-        pending.append(c)
-    ow_copy.wait()
-    for o in range(1, levels):
-        src = lax.rem(me_l + levels - o, levels)
-        send(mbuf.at[src], mbuf.at[src], m_send.at[o], m_recv.at[src], (me_h, src)).wait_recv()
+        for index in range(groups + 1):
+            rows = pl.ds(index * GROUP, GROUP if index < groups else owned)
+            part = mbuf.at[src, rows, :]
+            send(part, part, m_send.at[o, index], m_recv.at[src, index], (me_h, src)).wait_recv()
     gated = mbuf[0, :seqs, :]
     for l in range(1, levels):
         gated += mbuf[l, :seqs, :]
@@ -228,7 +251,7 @@
     tail0 = 2 * key_dim + 2 * val_dim
     return pl.pallas_call(
         functools.partial(kernel, heads, levels, in_gain.shape[0], (key_dim, val_dim, level_total, level_here)),
-        out_shape=jax.ShapeDtypeStruct((out_rows, out_cols), f32),
+        out_shape=pltpu.VMEM((out_rows, out_cols), f32),
         in_specs=[anyspace, vmem, anyspace, vmem, anyspace, vmem, vmem, anyspace],
         out_specs=vmem,
         scratch_shapes=[
@@ -249,7 +272,7 @@
             dma(()), dma((heads,)), dma((seqs // GROUP,)), dma(()),
             dma((heads,)), dma((heads,)),
             dma((levels,)), dma((levels,)), dma((levels,)), dma((levels,)),
-            dma((levels,)), dma((levels,)),
+            dma((levels, seqs // GROUP + 1)), dma((levels, seqs // GROUP + 1)),
             dma((heads,)), dma((heads,)),
         ],
         compiler_params=pltpu.CompilerParams(collective_id=0, has_side_effects=True),

time: 33.3 us -> 29.8 us (0.89)
  Pallas kernels: 31.7 us -> 29 us
  local copies, waits for them, and re-layouts: 1.38 us -> 0.62 us
    pallas_call x1, Pallas kernels: 31.7 us -> 29 us  [body(): pl.pallas_call(functools.partial(kernel, heads, levels, in_gain.shape[0],...]
    unnamed x1, local copies, waits for them, and re-layouts: 1.38 us -> 0.62 us
where the time goes in v2:
time: 29.8 us; the launch traced here: 29.6 us
  Pallas kernels  29 us (97%)
  local copies, waits for them, and re-layouts  0.62 us (2%)
    pallas_call x1, Pallas kernels, body(): pl.pallas_call(functools.partial(kernel, heads, levels, in_gain.shape[0],...  29 us
    unnamed x1, local copies, waits for them, and re-layouts  0.62 us

profile of v2, /device:TPU:0, one launch (start us, length us, event | category | flops | bytes accessed | tf_op | source)
XLA Modules:
  0.0 29.6 jit_solution(7953471687152965314)
XLA Ops:
  0.0 29.0 %shard_map.82 = f32[8,1024]{1,0:T(8,128)S(1)} custom-call(f32[64,128]{1,0:T(8,128)} %feat.1, f32[32,128]{1,0:T(8,128)} %bitcast.7, bf16[536,4096]{1,0:T(8,128)(2,1)} %bitcast.6, f32[1,24]{1,0:T(1,128)} %bias.1, bf16[64,768,128]{2,1,0:T(8,128)(2,1)} %bitcast.5, s32[1,64]{1,0:T(1,128)} %bitcast.8, f32[1,128]{1,0:T(1,128)} %bitcast.9, bf16[128,1024]{1,0:T(8,128)(2,1)} %outw.1), custom_call_target="tpu_custom_call" | custom-call | tf_op jit(solution)/shard_map/pallas_call | solution.py:252
  29.0 0.6 %copy.10 = f32[8,1024]{1,0:T(8,128)} copy(f32[8,1024]{1,0:T(8,128)S(1)} %shard_map.82) | data formatting | bytes 65536

commit v3 on v2

--- a/solution.py
+++ b/solution.py
@@ -25,9 +25,9 @@
 def kernel(
     heads, levels, width, dims,
     feat, gain, inw, bias, states, pos, ogain, outw, out,
-    xbuf, wbuf, sbuf, owbuf, proj, abuf, bbuf, mbuf, osend, orecv, qfull, wnorm, qw, biasbuf,
+    xbuf, wbuf, sbuf, owbuf, proj, abuf, bbuf, mbuf, osend, orecv, qfull, wnorm, qw, biasbuf, qsum,
     x_sem, w_sem, s_sem, ow_sem, p1_send, p1_recv, a_send, a_recv, b_send, b_recv,
-    m_send, m_recv, o_send, o_recv,
+    m_send, m_recv, o_send, o_recv, q_send, q_recv,
 ):
     key_dim, val_dim, level_total, level_here = dims
     seqs, fw = feat.shape
@@ -81,20 +81,28 @@
     def feature_wait(block):
         send(xbuf.at[block], xbuf.at[block], p1_send.at[0], p1_recv.at[block], (buddy, me_l)).wait_recv()
 
-    same = [lax.rem(me_h + o, heads) for o in range(2, heads, 2)]
-    for i, peer in enumerate(same):
+    chips, core = heads // 2, lax.rem(me_h, 2)
+    mirror_chip = chips - 1 - me_h // 2
+    skip = lax.rem(me_h // 2 - mirror_chip + chips, chips)
+    mirror = 2 * mirror_chip + core
+    direct = []
+    for j in range(1, chips - 1):
+        near = 2 * lax.rem(mirror_chip + j + (j + chips - skip) // chips, chips)
+        direct += [near + core, near + 1 - core]
+    feature_send(me_h, mirror, heads - 1)
+    for i, peer in enumerate(direct):
         feature_send(me_h, peer, i)
-    feature_send(me_h, buddy, heads - 1)
+    feature_send(me_h, buddy, heads - 2)
     for c in w_copies:
         c.wait()
     acc = jnp.zeros((seqs, cols), jnp.float32)
     squares = jnp.zeros((seqs, 1), jnp.float32)
-    other = [lax.rem(buddy + o, heads) for o in range(2, heads, 2)]
-    for i, src in enumerate([me_h, buddy] + same + other):
+    arrivals = [me_h, buddy, mirror] + direct + [2 * mirror_chip + 1 - core]
+    for i, src in enumerate(arrivals):
         if i:
             feature_wait(src)
-        if 2 <= i < 2 + len(same):
-            feature_send(src, buddy, len(same) + i - 2)
+        if i == 2:
+            feature_send(mirror, buddy, heads - 3)
         x = xbuf[src]
         g = gain[pl.ds(src * levels + me_l, 1), :]
         acc += lax.dot_general(
@@ -214,22 +222,30 @@
     gated = gated * jnp.concatenate([mbuf[l, seqs:, :] for l in range(levels)], axis=0)
     total_sq = jnp.sum(gated * gated, axis=1, keepdims=True)
     product = jnp.dot((gated * ogain[...]).astype(jnp.bfloat16), owbuf[...], preferred_element_type=jnp.float32)
-    wide_sq = jnp.broadcast_to(total_sq, (seqs, LANES))
+    qsum[me_h] = jnp.sum(jnp.where(row == col, jnp.broadcast_to(total_sq, (seqs, seqs)), 0.0), axis=0, keepdims=True)
     for h in range(heads):
-        osend[h, :, :out_cols] = product[h * out_rows : (h + 1) * out_rows]
-        osend[h, :, out_cols:] = wide_sq[h * out_rows : (h + 1) * out_rows]
+        osend[h] = product[h * out_rows : (h + 1) * out_rows]
     for o in range(1, heads):
         peer = lax.rem(me_h + o, heads)
         c = send(osend.at[peer], orecv.at[me_h], o_send.at[o], o_recv.at[me_h], (peer, me_l))
+        c.start()
+        pending.append(c)
+        c = send(qsum.at[me_h], qsum.at[me_h], q_send.at[o], q_recv.at[me_h], (peer, me_l))
         c.start()
         pending.append(c)
     total = osend[me_h]
     for o in range(1, heads):
         src = lax.rem(me_h + heads - o, heads)
         send(osend.at[src], orecv.at[src], o_send.at[o], o_recv.at[src], (src, me_l)).wait_recv()
+        send(qsum.at[src], qsum.at[src], q_send.at[o], q_recv.at[src], (src, me_l)).wait_recv()
         total += orecv[src]
-    mean = total[:, out_cols : out_cols + 1] / (heads * val_dim)
-    out[...] = total[:, :out_cols] * lax.rsqrt(mean + 1e-05)
+    all_sq = qsum[0]
+    for h in range(1, heads):
+        all_sq += qsum[h]
+    here = lax.broadcasted_iota(jnp.int32, (out_rows, seqs), 0) + me_h * out_rows
+    pick = lax.broadcasted_iota(jnp.int32, (out_rows, seqs), 1) == here
+    mean = jnp.sum(jnp.where(pick, jnp.broadcast_to(all_sq, pick.shape), 0.0), axis=1, keepdims=True) / (heads * val_dim)
+    out[...] = total * lax.rsqrt(mean + 1e-05)
     for c in pending:
         c.wait_send()
 
@@ -263,17 +279,18 @@
             pltpu.VMEM((levels, seqs + seqs // slots, key_dim), f32),
             pltpu.VMEM((levels, owned, tail0 - key_dim), f32),
             pltpu.VMEM((levels, seqs + owned, val_dim), f32),
-            pltpu.VMEM((heads, out_rows, out_cols + LANES), f32),
-            pltpu.VMEM((heads, out_rows, out_cols + LANES), f32),
+            pltpu.VMEM((heads, out_rows, out_cols), f32),
+            pltpu.VMEM((heads, out_rows, out_cols), f32),
             pltpu.VMEM((seqs, key_dim), f32),
             pltpu.VMEM((seqs, 2 * LANES), f32),
             pltpu.VMEM((seqs, level_here * key_dim), bf16),
             pltpu.VMEM((1, LANES), f32),
+            pltpu.VMEM((heads, 1, seqs), f32),
             dma(()), dma((heads,)), dma((seqs // GROUP,)), dma(()),
             dma((heads,)), dma((heads,)),
             dma((levels,)), dma((levels,)), dma((levels,)), dma((levels,)),
             dma((levels, seqs // GROUP + 1)), dma((levels, seqs // GROUP + 1)),
-            dma((heads,)), dma((heads,)),
+            dma((heads,)), dma((heads,)), dma((heads,)), dma((heads,)),
         ],
         compiler_params=pltpu.CompilerParams(collective_id=0, has_side_effects=True),
     )(

time: 29.8 us -> 29.3 us (0.983)
  Pallas kernels: 29 us -> 28.5 us
    pallas_call x1, Pallas kernels: 29 us -> 28.5 us  [body(): pl.pallas_call(functools.partial(kernel, heads, levels, in_gain.shape[0],...]
where the time goes in v3:
time: 29.3 us; the launch traced here: 29.2 us
  Pallas kernels  28.5 us (97%)
  local copies, waits for them, and re-layouts  0.62 us (2%)
    pallas_call x1, Pallas kernels, body(): pl.pallas_call(functools.partial(kernel, heads, levels, in_gain.shape[0],...  28.5 us
    unnamed x1, local copies, waits for them, and re-layouts  0.62 us

profile of v3, /device:TPU:0, one launch (start us, length us, event | category | flops | bytes accessed | tf_op | source)
XLA Modules:
  0.0 29.2 jit_solution(18120166106057866654)
XLA Ops:
  0.0 28.5 %shard_map.82 = f32[8,1024]{1,0:T(8,128)S(1)} custom-call(f32[64,128]{1,0:T(8,128)} %feat.1, f32[32,128]{1,0:T(8,128)} %bitcast.7, bf16[536,4096]{1,0:T(8,128)(2,1)} %bitcast.6, f32[1,24]{1,0:T(1,128)} %bias.1, bf16[64,768,128]{2,1,0:T(8,128)(2,1)} %bitcast.5, s32[1,64]{1,0:T(1,128)} %bitcast.8, f32[1,128]{1,0:T(1,128)} %bitcast.9, bf16[128,1024]{1,0:T(8,128)(2,1)} %outw.1), custom_call_target="tpu_custom_call" | custom-call | tf_op jit(solution)/shard_map/pallas_call | solution.py:268
  28.5 0.6 %copy.10 = f32[8,1024]{1,0:T(8,128)} copy(f32[8,1024]{1,0:T(8,128)S(1)} %shard_map.82) | data formatting | bytes 65536
